TPU v7x, 32 devices: a whole 2x2x4 slice. The times are simulated.
32 devices in a mesh: rep: 8 (over y, x, core), grp: 4 (over z).
Axes of the slice: x: 2, y: 2, z: 4, core: 2. Of those that a mesh axis runs over, the one named last changes fastest.
Arguments:
- tokens: bfloat16 [8, 1024, 512], P('rep', 'grp'), may hold values from -6 to 6
- segments: int32 [8, 1024], P('rep', 'grp'), may hold values from 0 to 1024, as said below
- positions: int32 [8, 1024], P('rep', 'grp'), may hold values from 0 to 1023, as said below
- norm1_gain: bfloat16 [512], P('grp'), may hold values from 0.5 to 1.5
- w_query: bfloat16 [512, 512], P('grp'), may hold values from -0.25 to 0.25
- w_key: bfloat16 [512, 512], P('grp'), may hold values from -0.25 to 0.25
- w_value: bfloat16 [512, 512], P('grp'), may hold values from -0.25 to 0.25
- w_out: bfloat16 [512, 512], P('grp'), may hold values from -1 to 1
- norm2_gain: bfloat16 [512], P('grp'), may hold values from 0.5 to 1.5
- w_gate: bfloat16 [512, 1376], P('grp'), may hold values from -0.25 to 0.25
- w_up: bfloat16 [512, 1376], P('grp'), may hold values from -0.25 to 0.25
- w_down: bfloat16 [1376, 512], P('grp'), may hold values from -0.15625 to 0.15625
- cotangent: bfloat16 [8, 1024, 512], P('rep', 'grp'), may hold values from -6 to 6
Outputs:
- output: bfloat16 [8, 1024, 512], P('rep', 'grp')
- input_grad: float32 [8, 1024, 512], P('rep', 'grp')
- grad_norm1: float32 [512], P('grp')
- grad_query: float32 [512, 512], P('grp')
- grad_key: float32 [512, 512], P('grp')
- grad_value: float32 [512, 512], P('grp')
- grad_out: float32 [512, 512], P('grp')
- grad_norm2: float32 [512], P('grp')
- grad_gate: float32 [512, 1376], P('grp')
- grad_up: float32 [512, 1376], P('grp')
- grad_down: float32 [1376, 512], P('grp')
Inputs may be any that keep to these rules, and one draw needn't show every extreme that they name: `segments`: in each sequence the documents are runs of consecutive tokens numbered 1, 2, 3 in order; tokens after the last document, if any, are padding numbered 0. `positions`: A token's index in its sequence minus the index of the first token of its run (its document, or the padding).
All inputs are finite; a program needn't handle non-finite values.
Results may differ from a plain program's by a relative error of at most 0.019.
Values may be sent and summed in bfloat16 or wider, within the bound.
No kernel may reach another device: no remote copies, remote signals or barrier semaphores. Data moves between devices by JAX's collectives and lax.ppermute only.
A program may use at most 64 MiB of HBM per device.

v0:
```python
import jax
import jax.numpy as jnp
from jax import lax
from jax.sharding import PartitionSpec as P

D = 512
H = 8
KV = 8
HD = 64
EPSILON = 1e-05
NEGATIVE = -1e30


def norm_scale(values):
    return lax.rsqrt(jnp.mean(values * values, axis=-1, keepdims=True) + EPSILON)


def rotation_tables(positions, width):
    halves = width // 2
    frequency = 10000.0 ** (-2.0 * jnp.arange(halves, dtype=jnp.float32) / width)
    angles = positions.astype(jnp.float32)[..., None, None] * frequency
    return (jnp.cos(angles), jnp.sin(angles))


def rotate(values, cosine, sines):
    halves = values.shape[-1] // 2
    first_half = values[..., :halves]
    second_half = values[..., halves:]
    return jnp.concatenate(
        [first_half * cosine - second_half * sines, second_half * cosine + first_half * sines],
        axis=-1,
    )


def rotate_back(gradient, cosine, sines):
    halves = gradient.shape[-1] // 2
    first_half = gradient[..., :halves]
    second_half = gradient[..., halves:]
    return jnp.concatenate(
        [first_half * cosine + second_half * sines, second_half * cosine - first_half * sines],
        axis=-1,
    )


def contract_rows(left, right):
    return lax.dot_general(
        left, right, (((0,), (0,)), ((), ())), preferred_element_type=jnp.float32
    )


def against(left, right):
    return lax.dot_general(
        left, right, (((1,), (1,)), ((), ())), preferred_element_type=jnp.float32
    )


def fetch_attention(norm1_gain, w_query, w_key, w_value, w_out):
    return (
        lax.all_gather(norm1_gain, "grp", axis=0, tiled=True),
        lax.all_gather(w_query, "grp", axis=0, tiled=True),
        lax.all_gather(w_key, "grp", axis=0, tiled=True),
        lax.all_gather(w_value, "grp", axis=0, tiled=True),
        lax.all_gather(w_out, "grp", axis=0, tiled=True),
    )


def fetch_mlp(norm2_gain, w_gate, w_up, w_down):
    return (
        lax.all_gather(norm2_gain, "grp", axis=0, tiled=True),
        lax.all_gather(w_gate, "grp", axis=0, tiled=True),
        lax.all_gather(w_up, "grp", axis=0, tiled=True),
        lax.all_gather(w_down, "grp", axis=0, tiled=True),
    )


def replica_all(parts):
    return (
        lax.psum(parts[0].astype(jnp.bfloat16), "rep").astype(jnp.float32),
        lax.psum(parts[1].astype(jnp.bfloat16), "rep").astype(jnp.float32),
        lax.psum(parts[2].astype(jnp.bfloat16), "rep").astype(jnp.float32),
        lax.psum(parts[3].astype(jnp.bfloat16), "rep").astype(jnp.float32),
        lax.psum(parts[4].astype(jnp.bfloat16), "rep").astype(jnp.float32),
        lax.psum(parts[5].astype(jnp.bfloat16), "rep").astype(jnp.float32),
        lax.psum(parts[6].astype(jnp.bfloat16), "rep").astype(jnp.float32),
        lax.psum(parts[7].astype(jnp.bfloat16), "rep").astype(jnp.float32),
        lax.psum(parts[8].astype(jnp.bfloat16), "rep").astype(jnp.float32),
    )


def flat_body(
    tokens,
    segments,
    positions,
    norm1_gain,
    w_query,
    w_key,
    w_value,
    w_out,
    norm2_gain,
    w_gate,
    w_up,
    w_down,
    cotangent,
):
    seq_count = tokens.shape[0]
    local_len = tokens.shape[1]
    full_len = local_len * lax.axis_size("grp")
    row_count = seq_count * local_len
    group_size = H // KV
    score_scale = HD ** (-0.5)
    inputs = tokens.reshape(row_count, D).astype(jnp.float32)
    gain_in, query_full, key_full, value_full, out_full = fetch_attention(
        norm1_gain, w_query, w_key, w_value, w_out
    )
    scale_in = norm_scale(inputs)
    unit_in = inputs * scale_in
    normed_in = (unit_in * gain_in.astype(jnp.float32)).astype(jnp.bfloat16)
    query_raw = jnp.dot(normed_in, query_full, preferred_element_type=jnp.float32)
    key_raw = jnp.dot(normed_in, key_full, preferred_element_type=jnp.float32)
    value_raw = jnp.dot(normed_in, value_full, preferred_element_type=jnp.float32)
    cosine, sines = rotation_tables(positions, HD)
    query_rot = rotate(query_raw.reshape(seq_count, local_len, H, HD), cosine, sines).astype(
        jnp.bfloat16
    )
    key_rot = (
        rotate(key_raw.reshape(seq_count, local_len, KV, HD), cosine, sines)
        .astype(jnp.bfloat16)
        .reshape(seq_count, local_len, KV * HD)
    )
    value_low = value_raw.astype(jnp.bfloat16).reshape(seq_count, local_len, KV * HD)
    keys_all, values_all = (
        lax.all_gather(key_rot, "grp", axis=1, tiled=True),
        lax.all_gather(value_low, "grp", axis=1, tiled=True),
    )
    query_index = lax.axis_index("grp") * local_len + jnp.arange(local_len, dtype=jnp.int32)
    offsets = query_index[:, None] - jnp.arange(full_len, dtype=jnp.int32)[None, :]
    allowed = (
        (offsets >= 0)[None]
        & (offsets[None] <= positions[:, :, None])
        & ((segments[:, :, None] != 0) | (offsets == 0)[None])
    )
    query_heads = query_rot.reshape(seq_count, local_len, KV, group_size, HD).transpose(
        2, 0, 1, 3, 4
    )
    key_heads = keys_all.reshape(seq_count, full_len, KV, HD).transpose(2, 0, 1, 3)
    value_heads = values_all.reshape(seq_count, full_len, KV, HD).transpose(2, 0, 1, 3)

    def masked_scores(query_head, key_head):
        scores = (
            jnp.einsum("bqgd,bjd->bgqj", query_head, key_head, preferred_element_type=jnp.float32)
            * score_scale
        )
        return jnp.where(allowed[:, None], scores, NEGATIVE)

    def head_forward(items):
        query_head, key_head, value_head = items
        masked = masked_scores(query_head, key_head)
        peak = jnp.max(masked, axis=-1, keepdims=True)
        exponent = jnp.exp(masked - peak)
        summed = jnp.sum(exponent, axis=-1, keepdims=True)
        softmaxed = exponent / summed
        attended = jnp.einsum(
            "bgqj,bjd->bqgd",
            softmaxed.astype(jnp.bfloat16),
            value_head,
            preferred_element_type=jnp.float32,
        )
        return (attended, peak + jnp.log(summed))

    attended, log_totals = lax.map(head_forward, (query_heads, key_heads, value_heads))
    attn_low = attended.transpose(1, 2, 0, 3, 4).reshape(row_count, H * HD).astype(jnp.bfloat16)
    middle = inputs + jnp.dot(attn_low, out_full, preferred_element_type=jnp.float32)
    gain_mid, gate_full, up_full, down_full = fetch_mlp(norm2_gain, w_gate, w_up, w_down)
    scale_mid = norm_scale(middle)
    unit_mid = middle * scale_mid
    normed_mid = (unit_mid * gain_mid.astype(jnp.float32)).astype(jnp.bfloat16)
    gate_raw = jnp.dot(normed_mid, gate_full, preferred_element_type=jnp.float32)
    up_raw = jnp.dot(normed_mid, up_full, preferred_element_type=jnp.float32)
    sigmoid_gate = jax.nn.sigmoid(gate_raw)
    hidden_low = (gate_raw * sigmoid_gate * up_raw).astype(jnp.bfloat16)
    output = (
        (middle + jnp.dot(hidden_low, down_full, preferred_element_type=jnp.float32))
        .astype(jnp.bfloat16)
        .reshape(tokens.shape)
    )
    gain_mid, gate_full, up_full, down_full = fetch_mlp(norm2_gain, w_gate, w_up, w_down)
    cot_low = cotangent.reshape(row_count, D)
    hidden_delta = against(cot_low, down_full)
    gate_delta = (
        hidden_delta * up_raw * sigmoid_gate * (1.0 + gate_raw * (1.0 - sigmoid_gate))
    ).astype(jnp.bfloat16)
    upward_delta = (hidden_delta * gate_raw * sigmoid_gate).astype(jnp.bfloat16)
    columns = normed_mid
    gate_part = lax.psum_scatter(
        contract_rows(columns, gate_delta).astype(jnp.bfloat16),
        "grp",
        scatter_dimension=0,
        tiled=True,
    ).astype(jnp.float32)
    columns = normed_mid
    up_part = lax.psum_scatter(
        contract_rows(columns, upward_delta).astype(jnp.bfloat16),
        "grp",
        scatter_dimension=0,
        tiled=True,
    ).astype(jnp.float32)
    columns = hidden_low
    down_part = lax.psum_scatter(
        contract_rows(columns, cot_low).astype(jnp.bfloat16), "grp", scatter_dimension=0, tiled=True
    ).astype(jnp.float32)
    gate_grad, up_grad, down_grad = (gate_part, up_part, down_part)
    normed_mid_delta = against(gate_delta, gate_full) + against(upward_delta, up_full)
    gain_mid_term = jnp.sum(normed_mid_delta * unit_mid, axis=0)
    scaled_mid = normed_mid_delta * gain_mid.astype(jnp.float32)
    middle_delta = cot_low.astype(jnp.float32) + scale_mid * (
        scaled_mid - unit_mid * jnp.mean(scaled_mid * unit_mid, axis=-1, keepdims=True)
    )
    gain_in, query_full, key_full, value_full, out_full = fetch_attention(
        norm1_gain, w_query, w_key, w_value, w_out
    )
    out_delta = middle_delta.astype(jnp.bfloat16)
    out_term = contract_rows(attn_low, out_delta)
    attn_delta = against(out_delta, out_full).astype(jnp.bfloat16)
    attn_heads = attn_delta.reshape(seq_count, local_len, KV, group_size, HD).transpose(
        2, 0, 1, 3, 4
    )

    def head_backward(items):
        query_head, key_head, value_head, log_total, attn_head = items
        masked = masked_scores(query_head, key_head)
        softmaxed = jnp.exp(masked - log_total)
        prob_delta = jnp.einsum(
            "bqgd,bjd->bgqj", attn_head, value_head, preferred_element_type=jnp.float32
        )
        value_delta = jnp.einsum(
            "bgqj,bqgd->bjd",
            softmaxed.astype(jnp.bfloat16),
            attn_head,
            preferred_element_type=jnp.float32,
        )
        score_delta = (
            softmaxed * (prob_delta - jnp.sum(softmaxed * prob_delta, axis=-1, keepdims=True))
        ).astype(jnp.bfloat16)
        query_delta = (
            jnp.einsum("bgqj,bjd->bqgd", score_delta, key_head, preferred_element_type=jnp.float32)
            * score_scale
        )
        key_delta = (
            jnp.einsum(
                "bgqj,bqgd->bjd", score_delta, query_head, preferred_element_type=jnp.float32
            )
            * score_scale
        )
        return (query_delta, key_delta, value_delta)

    query_deltas, key_deltas, value_deltas = lax.map(
        head_backward, (query_heads, key_heads, value_heads, log_totals, attn_heads)
    )
    key_delta_all = key_deltas.transpose(1, 2, 0, 3).reshape(seq_count, full_len, KV * HD)
    value_delta_all = value_deltas.transpose(1, 2, 0, 3).reshape(seq_count, full_len, KV * HD)
    key_delta_own, value_delta_own = (
        lax.psum_scatter(
            key_delta_all.astype(jnp.bfloat16), "grp", scatter_dimension=1, tiled=True
        ).astype(jnp.float32),
        lax.psum_scatter(
            value_delta_all.astype(jnp.bfloat16), "grp", scatter_dimension=1, tiled=True
        ).astype(jnp.float32),
    )
    query_low = (
        rotate_back(
            query_deltas.transpose(1, 2, 0, 3, 4).reshape(seq_count, local_len, H, HD),
            cosine,
            sines,
        )
        .reshape(row_count, H * HD)
        .astype(jnp.bfloat16)
    )
    key_low = (
        rotate_back(key_delta_own.reshape(seq_count, local_len, KV, HD), cosine, sines)
        .reshape(row_count, KV * HD)
        .astype(jnp.bfloat16)
    )
    value_delta_low = value_delta_own.reshape(row_count, KV * HD).astype(jnp.bfloat16)
    query_term = contract_rows(normed_in, query_low)
    key_term = contract_rows(normed_in, key_low)
    value_term = contract_rows(normed_in, value_delta_low)
    normed_in_delta = (
        against(query_low, query_full)
        + against(key_low, key_full)
        + against(value_delta_low, value_full)
    )
    gain_in_term = jnp.sum(normed_in_delta * unit_in, axis=0)
    scaled_in = normed_in_delta * gain_in.astype(jnp.float32)
    input_grad = middle_delta + scale_in * (
        scaled_in - unit_in * jnp.mean(scaled_in * unit_in, axis=-1, keepdims=True)
    )
    norm1_part, norm2_part, query_part, key_part, value_part, out_part = (
        lax.psum_scatter(
            gain_in_term.astype(jnp.bfloat16), "grp", scatter_dimension=0, tiled=True
        ).astype(jnp.float32),
        lax.psum_scatter(
            gain_mid_term.astype(jnp.bfloat16), "grp", scatter_dimension=0, tiled=True
        ).astype(jnp.float32),
        lax.psum_scatter(
            query_term.astype(jnp.bfloat16), "grp", scatter_dimension=0, tiled=True
        ).astype(jnp.float32),
        lax.psum_scatter(
            key_term.astype(jnp.bfloat16), "grp", scatter_dimension=0, tiled=True
        ).astype(jnp.float32),
        lax.psum_scatter(
            value_term.astype(jnp.bfloat16), "grp", scatter_dimension=0, tiled=True
        ).astype(jnp.float32),
        lax.psum_scatter(
            out_term.astype(jnp.bfloat16), "grp", scatter_dimension=0, tiled=True
        ).astype(jnp.float32),
    )
    (
        norm1_grad,
        norm2_grad,
        query_grad,
        key_grad,
        value_grad,
        out_grad,
        gate_grad,
        up_grad,
        down_grad,
    ) = replica_all(
        (
            norm1_part,
            norm2_part,
            query_part,
            key_part,
            value_part,
            out_part,
            gate_grad,
            up_grad,
            down_grad,
        )
    )
    return (
        output,
        input_grad.reshape(tokens.shape),
        norm1_grad,
        query_grad,
        key_grad,
        value_grad,
        out_grad,
        norm2_grad,
        gate_grad,
        up_grad,
        down_grad,
    )


def on_device(
    tokens,
    segments,
    positions,
    norm1_gain,
    w_query,
    w_key,
    w_value,
    w_out,
    norm2_gain,
    w_gate,
    w_up,
    w_down,
    cotangent,
):
    results = flat_body(
        tokens,
        segments,
        positions,
        norm1_gain,
        w_query,
        w_key,
        w_value,
        w_out,
        norm2_gain,
        w_gate,
        w_up,
        w_down,
        cotangent,
    )
    return results


def solution(mesh):
    in_specs = (
        P("rep", "grp", None),
        P("rep", "grp"),
        P("rep", "grp"),
        P("grp"),
        P("grp", None),
        P("grp", None),
        P("grp", None),
        P("grp", None),
        P("grp"),
        P("grp", None),
        P("grp", None),
        P("grp", None),
        P("rep", "grp", None),
    )
    out_specs = (
        P("rep", "grp", None),
        P("rep", "grp", None),
        P("grp"),
        P("grp", None),
        P("grp", None),
        P("grp", None),
        P("grp", None),
        P("grp"),
        P("grp", None),
        P("grp", None),
        P("grp", None),
    )
    return jax.shard_map(
        on_device, mesh=mesh, in_specs=in_specs, out_specs=out_specs, check_vma=False
    )
```

profile of v0, /device:TPU:0, one launch (start us, length us, event | category | flops | bytes accessed | tf_op | source)
XLA Modules:
  0.0 614.8 jit_solution(3722437577382787025)
XLA Ops:
  7.2 17.6 %all_gather.43 = bf16[512,512]{1,0:T(8,128)(2,1)S(1)} all-gather(bf16[128,512]{1,0:T(8,128)(2,1)} %param.23), channel_id=1, replica_groups=mesh['rep'=8,'grp'=4] {'grp'}, dimensions={0}, use_global_device_ids=true | all-gather | bytes 655360 | tf_op jit(solution)/shard_map/all_gather | solution.py:62
  24.8 11.8 %all-gather.1 = bf16[4,1,128]{2,1,0:T(2,128)(2,1)S(1)} all-gather(bf16[1,1,128]{2,1,0:T(2,128)(2,1)} %bitcast.349), channel_id=1, replica_groups=mesh['rep'=8,'grp'=4] {'grp'}, dimensions={0}, use_global_device_ids=true | all-gather | bytes 1280 | tf_op jit(solution)/shard_map/all_gather | solution.py:59
  37.8 2.0 convolution_convert_fusion.8
  39.9 19.2 %all_gather.47 = bf16[512,512]{1,0:T(8,128)(2,1)S(1)} all-gather(bf16[128,512]{1,0:T(8,128)(2,1)S(1)} %copy-done.27), channel_id=1, replica_groups=mesh['rep'=8,'grp'=4] {'grp'}, dimensions={0}, use_global_device_ids=true | all-gather | bytes 655360 | tf_op jit(solution)/shard_map/all_gather | solution.py:60
  59.4 19.7 %all_gather.45 = bf16[512,512]{1,0:T(8,128)(2,1)S(1)} all-gather(bf16[128,512]{1,0:T(8,128)(2,1)S(1)} %copy-done.28), channel_id=1, replica_groups=mesh['rep'=8,'grp'=4] {'grp'}, dimensions={0}, use_global_device_ids=true | all-gather | bytes 655360 | tf_op jit(solution)/shard_map/all_gather | solution.py:61
  84.0 17.9 %all_gather.48 = bf16[512,512]{1,0:T(8,128)(2,1)S(1)} all-gather(bf16[128,512]{1,0:T(8,128)(2,1)S(1)} %copy-done.29), channel_id=1, replica_groups=mesh['rep'=8,'grp'=4] {'grp'}, dimensions={0}, use_global_device_ids=true | all-gather | bytes 655360 | tf_op jit(solution)/shard_map/all_gather | solution.py:63
  101.9 9.7 %all-gather.2 = bf16[4,1,128]{2,1,0:T(2,128)(2,1)S(1)} all-gather(bf16[1,1,128]{2,1,0:T(2,128)(2,1)S(1)} %bitcast.350), channel_id=1, replica_groups=mesh['rep'=8,'grp'=4] {'grp'}, dimensions={0}, use_global_device_ids=true | all-gather | bytes 1280 | tf_op jit(solution)/shard_map/all_gather | solution.py:69
  112.3 2.3 copy.43
  114.6 2.0 copy.46
  116.7 2.7 copy.47
  119.4 26.0 %while.30 = (s32[]{:T(128)}, bf16[8,1,256,1,64]{2,4,3,1,0:T(8,128)(2,1)}, f32[8,1,1,256,1]{3,4,2,1,0:T(1,128)}, bf16[8,1,1024,64]{3,2,1,0:T(8,128)(2,1)S(1)}, bf...) while((s32[]{:T(128)}, ...), condition=%wide.region_4.5_spmd.clone.clone, body=%wide.region_1.4_spmd.clone.sunk.clone | while | flops 71040768 | bytes 3783017 | solution.py:170
  148.5 3.0 fusion.103
  151.6 31.7 %all-gather.13.cloned.1.call-done = bf16[512,1376]{0,1:T(8,128)(2,1)} async-done(((bf16[128,1376]{0,1:T(8,128)(2,1)}), bf16[512,1376]{0,1:T(8,128)(2,1)}) %all-gather.13.cloned.1.call-update) | async-done | bytes 1409040 | tf_op jit(solution)/shard_map/all_gather | solution.py:71
  183.2 3.0 fusion.104
  186.2 30.8 %all-gather.15.cloned.1.call-done = bf16[1376,512]{1,0:T(8,128)(2,1)} async-done(((bf16[344,512]{1,0:T(8,128)(2,1)}), bf16[1376,512]{1,0:T(8,128)(2,1)}) %all-gather.15.cloned.1.call-update) | async-done | bytes 1409040 | tf_op jit(solution)/shard_map/all_gather | solution.py:72
  217.1 4.0 multiply_convert_fusion.1
  226.2 60.1 %while.31 = (s32[]{:T(128)}, f32[8,1,256,1,64]{2,4,3,1,0:T(8,128)S(1)}, bf16[8,1,1024,64]{2,3,1,0:T(8,128)(2,1)}, bf16[8,1,1024,64]{2,3,1,0:T(8,128)(2,1)}, bf16...) while((s32[]{:T(128)}, ...), condition=%wide.region_9.10_spmd.clone.clone, body=%wide.region_7.9_spmd.clone.sunk.clone | while | flops 172048128 | bytes 9384321 | solution.py:256
  231.1 1.7 fusion.188
  235.7 1.6 multiply_reduce_fusion.6
  238.7 1.7 fusion.188
  246.1 1.7 fusion.188
  250.6 1.7 multiply_reduce_fusion.6
  253.6 1.7 fusion.188
  261.2 1.7 fusion.188
  268.7 1.7 fusion.188
  273.2 1.6 multiply_reduce_fusion.6
  276.2 1.7 fusion.188
  283.7 1.7 fusion.188
  290.4 1.7 convolution_convert_fusion
  296.0 1.7 convolution_convert_fusion.2
  297.7 15.1 %reduce-scatter.14.cloned.1.call-done = bf16[1,256,512]{1,2,0:T(8,128)(2,1)} async-done(((bf16[1,1024,512]{1,2,0:T(8,128)(2,1)}), bf16[1,256,512]{1,2,0:T(8,128)(2,1)}) %reduce-scatter.14.cloned.1.call-update) | async-done | bytes 262160 | tf_op jit(solution)/shard_map/reduce_scatter | solution.py:262
  317.7 23.2 %reduce-scatter.16.cloned.1.call-done = bf16[1,256,512]{1,2,0:T(8,128)(2,1)} async-done(((bf16[1,1024,512]{1,2,0:T(8,128)(2,1)}), bf16[1,256,512]{1,2,0:T(8,128)(2,1)}) %reduce-scatter.16.cloned.1.call-update) | async-done | bytes 262160 | tf_op jit(solution)/shard_map/reduce_scatter | solution.py:265
  340.9 2.2 convolution_convert_fusion.4
  344.4 2.7 fusion.63
  347.5 27.7 %reduce-scatter.28.cloned.1.call-done = bf16[128,1376]{1,0:T(8,128)(2,1)} async-done(((bf16[512,1376]{1,0:T(8,128)(2,1)}), bf16[128,1376]{1,0:T(8,128)(2,1)}) %reduce-scatter.28.cloned.1.call-update) | async-done | bytes 352272
  375.2 1.9 copy.56
  377.1 32.6 %reduce-scatter.30.cloned.1.call-done = bf16[128,1376]{1,0:T(8,128)(2,1)} async-done(((bf16[512,1376]{1,0:T(8,128)(2,1)}), bf16[128,1376]{1,0:T(8,128)(2,1)}) %reduce-scatter.30.cloned.1.call-update) | async-done | bytes 352272
  409.7 1.9 copy.58
  411.6 21.4 %reduce-scatter.24.cloned.1.call-done = bf16[128,512]{1,0:T(8,128)(2,1)} async-done(((bf16[512,512]{1,0:T(8,128)(2,1)}), bf16[128,512]{1,0:T(8,128)(2,1)}) %reduce-scatter.24.cloned.1.call-update) | async-done | bytes 131088 | tf_op jit(solution)/shard_map/reduce_scatter | solution.py:313
  433.1 33.5 %reduce-scatter.26.cloned.1.call-done = bf16[344,512]{1,0:T(8,128)(2,1)} async-done(((bf16[1376,512]{1,0:T(8,128)(2,1)}), bf16[344,512]{1,0:T(8,128)(2,1)}) %reduce-scatter.26.cloned.1.call-update) | async-done | bytes 352272 | tf_op jit(solution)/shard_map/reduce_scatter | solution.py:208
  466.5 23.4 %reduce-scatter.18.cloned.1.call-done = bf16[128,512]{1,0:T(8,128)(2,1)} async-done(((bf16[512,512]{1,0:T(8,128)(2,1)}), bf16[128,512]{1,0:T(8,128)(2,1)}) %reduce-scatter.18.cloned.1.call-update) | async-done | bytes 131088 | tf_op jit(solution)/shard_map/reduce_scatter | solution.py:304
  489.9 23.0 %reduce-scatter.20.cloned.1.call-done = bf16[128,512]{1,0:T(8,128)(2,1)} async-done(((bf16[512,512]{1,0:T(8,128)(2,1)}), bf16[128,512]{1,0:T(8,128)(2,1)}) %reduce-scatter.20.cloned.1.call-update) | async-done | bytes 131088 | tf_op jit(solution)/shard_map/reduce_scatter | solution.py:307
  512.9 22.9 %reduce-scatter.22.cloned.1.call-done = bf16[128,512]{1,0:T(8,128)(2,1)} async-done(((bf16[512,512]{1,0:T(8,128)(2,1)}), bf16[128,512]{1,0:T(8,128)(2,1)}) %reduce-scatter.22.cloned.1.call-update) | async-done | bytes 131088 | tf_op jit(solution)/shard_map/reduce_scatter | solution.py:310
  537.5 8.6 %all-reduce.4 = (bf16[512]{0:T(512)(128)(2,1)S(1)}, bf16[512]{0:T(512)(128)(2,1)S(1)}) all-reduce(bf16[512]{0:T(512)(128)(2,1)S(1)} %get-tuple-element.225, bf16[512]{0:T(512)(128)(2,1)S(1)} %copy-done.30), channel_id=5, replica_groups=mesh['rep'=8,'grp'=4] {'grp'}, use_global_device_ids=true, to_apply=%region_14.15.clone | all-reduce | flops 1024 | bytes 4096
  546.3 12.0 %all-reduce.2 = (bf16[128]{0:T(256)(128)(2,1)S(1)}, bf16[128]{0:T(256)(128)(2,1)S(1)}) all-reduce(bf16[128]{0:T(256)(128)(2,1)S(1)} %dynamic-slice.1, bf16[128]{0:T(256)(128)(2,1)S(1)} %dynamic-slice.3), channel_id=1, replica_groups=mesh['rep'=8,'grp'=4] {'rep'}, use_global_device_ids=true, to_apply=%region_15.16 | all-reduce | flops 256 | bytes 1024 | tf_op jit(solution)/shard_map/psum | solution.py:78
  560.3 38.6 %all-reduce.7.cloned.1.call-done = (bf16[128,512]{1,0:T(8,128)(2,1)}, bf16[128,512]{1,0:T(8,128)(2,1)}, bf16[128,512]{1,0:T(8,128)(2,1)}, bf16[128,512]{1,0:T(8,...) async-done(((bf16[128,512]{1,0:T(8,128)(2,1)}, bf16[128,512]{1,0:T(8,128)(2,1)}, bf16[128,512]{1,0:T(8,128)(2,1)}, ...) | async-done | bytes 1581072 | tf_op jit(solution)/shard_map/psum | solution.py:80
  598.9 1.7 convert_element_type.288
  602.2 1.7 convert_element_type.292
  (252 shorter events, 106.3 us)
Async XLA Ops:
  7.2 32.7 %copy-start.27 = (bf16[128,512]{1,0:T(8,128)(2,1)S(1)}, bf16[128,512]{1,0:T(8,128)(2,1)}, u32[]{:S(2)}) copy-start(bf16[128,512]{1,0:T(8,128)(2,1)} %param.21) | copy-start | bytes 393220
  7.2 105.1 %all-gather.17.cloned.1.call-start = ((), (), s32[]{:S(2)}) async-start(), calls=%async_computation.20 | async-start | bytes 1310720 | tf_op jit(solution)/shard_map/all_gather | solution.py:133
  24.8 15.0 %copy-start.14 = (bf16[512,512]{1,0:T(8,128)(2,1)}, bf16[512,512]{1,0:T(8,128)(2,1)S(1)}, u32[]{:S(2)}) copy-start(bf16[512,512]{1,0:T(8,128)(2,1)S(1)} %all_gather.43) | copy-start | bytes 1572868
  37.7 21.6 %copy-start.31 = (s32[1,256]{1,0:T(1,128)S(1)}, s32[1,256]{1,0:T(1,128)}, u32[]{:S(2)}) copy-start(s32[1,256]{1,0:T(1,128)} %param.19) | copy-start | bytes 3076
  37.8 21.6 %copy-start.28 = (bf16[128,512]{1,0:T(8,128)(2,1)S(1)}, bf16[128,512]{1,0:T(8,128)(2,1)}, u32[]{:S(2)}) copy-start(bf16[128,512]{1,0:T(8,128)(2,1)} %param.22) | copy-start | bytes 393220
  39.8 76.8 %all-gather.9.cloned.1.call-start = ((), (), s32[]{:S(2)}) async-start(), calls=%async_computation.9 | async-start | bytes 1310720 | tf_op jit(solution)/shard_map/all_gather | solution.py:132
  59.1 20.6 %copy-start.4 = (bf16[512,512]{1,0:T(8,128)(2,1)}, bf16[512,512]{1,0:T(8,128)(2,1)S(1)}, u32[]{:S(2)}) copy-start(bf16[512,512]{1,0:T(8,128)(2,1)S(1)} %all_gather.47) | copy-start | bytes 1572868
  59.1 20.2 %copy-start = (bf16[1,256,512]{2,1,0:T(8,128)(2,1)S(1)}, bf16[1,256,512]{2,1,0:T(8,128)(2,1)}, u32[]{:S(2)}) copy-start(bf16[1,256,512]{2,1,0:T(8,128)(2,1)} %param.17) | copy-start | bytes 786436
  80.3 2.3 copy-start.25
  80.5 3.5 copy-start.34
  80.5 3.5 copy-start.29
  80.5 21.4 %copy-start.33 = (bf16[128]{0:T(256)(128)(2,1)S(1)}, bf16[128]{0:T(256)(128)(2,1)}, u32[]{:S(2)}) copy-start(bf16[128]{0:T(256)(128)(2,1)} %param.25) | copy-start | bytes 772
  81.3 67.2 %all-gather.11.cloned.1.call-start = ((), (), s32[]{:S(2)}) async-start(), calls=%async_computation.10 | async-start | bytes 1761280 | tf_op jit(solution)/shard_map/all_gather | solution.py:70
  82.0 101.2 %all-gather.13.cloned.1.call-start = ((), (), s32[]{:S(2)}) async-start(), calls=%async_computation.11 | async-start | bytes 1761280 | tf_op jit(solution)/shard_map/all_gather | solution.py:71
  82.6 134.4 %all-gather.15.cloned.1.call-start = ((), (), s32[]{:S(2)}) async-start(), calls=%async_computation.12 | async-start | bytes 1761280 | tf_op jit(solution)/shard_map/all_gather | solution.py:72
  83.2 229.6 %reduce-scatter.14.cloned.1.call-start = ((), (), s32[]{:S(2)}) async-start(), calls=%async_computation.13 | async-start | bytes 1310720 | tf_op jit(solution)/shard_map/reduce_scatter | solution.py:262
  101.9 44.8 %copy-start.6 = (bf16[512,512]{1,0:T(8,128)(2,1)}, bf16[512,512]{1,0:T(8,128)(2,1)S(1)}, u32[]{:S(2)}) copy-start(bf16[512,512]{1,0:T(8,128)(2,1)S(1)} %all_gather.48) | copy-start | bytes 1572868
  145.4 1.3 copy-start.3
  145.4 6.1 copy-start.35
  145.4 6.1 copy-start.38
  151.6 65.5 %copy-start.16 = (bf16[1,256,512]{2,1,0:T(8,128)(2,1)S(1)}, bf16[1,256,512]{2,1,0:T(8,128)(2,1)}, u32[]{:S(2)}) copy-start(bf16[1,256,512]{2,1,0:T(8,128)(2,1)} %param.29) | copy-start | bytes 786436
  186.2 34.8 %copy-start.2 = (bf16[512,1376]{0,1:T(8,128)(2,1)S(1)}, bf16[512,1376]{0,1:T(8,128)(2,1)}, u32[]{:S(2)}) copy-start(bf16[512,1376]{0,1:T(8,128)(2,1)} %all-gather.11.cloned.1.call-done) | copy-start | bytes 4227076
  221.0 3.1 copy-start.8
  221.0 3.1 copy-start.10
  221.0 1.9 copy-start.1
  222.9 1.2 copy-start.17
  224.1 1.5 copy-start.32
  224.2 1.5 copy-start.36
  224.2 1.5 copy-start.39
  286.4 54.5 %reduce-scatter.16.cloned.1.call-start = ((), (), s32[]{:S(2)}) async-start(), calls=%async_computation.14 | async-start | bytes 1310720 | tf_op jit(solution)/shard_map/reduce_scatter | solution.py:265
  287.1 88.1 %reduce-scatter.28.cloned.1.call-start = ((), (), s32[]{:S(2)}) async-start(), calls=%async_computation.21 | async-start | bytes 1802240
  290.4 119.3 %reduce-scatter.30.cloned.1.call-start = ((), (), s32[]{:S(2)}) async-start(), calls=%async_computation.22 | async-start | bytes 1802240
  293.7 2.3 copy-start.9
  293.7 2.3 copy-start.18
  293.7 139.4 %reduce-scatter.24.cloned.1.call-start = ((), (), s32[]{:S(2)}) async-start(), calls=%async_computation.18 | async-start | bytes 655360 | tf_op jit(solution)/shard_map/reduce_scatter | solution.py:313
  295.7 170.8 %reduce-scatter.26.cloned.1.call-start = ((), (), s32[]{:S(2)}) async-start(), calls=%async_computation.19 | async-start | bytes 1761280 | tf_op jit(solution)/shard_map/reduce_scatter | solution.py:208
  297.6 16.2 %copy-start.26 = (f32[256,32]{0,1:T(8,128)S(1)}, f32[256,32]{0,1:T(8,128)}, u32[]{:S(2)}) copy-start(f32[256,32]{0,1:T(8,128)} %copy-done.25) | copy-start | bytes 98308
  297.7 192.2 %reduce-scatter.18.cloned.1.call-start = ((), (), s32[]{:S(2)}) async-start(), calls=%async_computation.15 | async-start | bytes 655360 | tf_op jit(solution)/shard_map/reduce_scatter | solution.py:304
  315.0 2.6 copy-start.11
  316.3 196.6 %reduce-scatter.20.cloned.1.call-start = ((), (), s32[]{:S(2)}) async-start(), calls=%async_computation.16 | async-start | bytes 655360 | tf_op jit(solution)/shard_map/reduce_scatter | solution.py:307
  316.4 26.8 %copy-start.37 = (u32[32]{0:T(128)S(1)}, u32[32]{0:T(128)}, u32[]{:S(2)}) copy-start(u32[32]{0:T(128)} %constant.83) | copy-start | bytes 388
  317.6 218.1 %reduce-scatter.22.cloned.1.call-start = ((), (), s32[]{:S(2)}) async-start(), calls=%async_computation.17 | async-start | bytes 655360 | tf_op jit(solution)/shard_map/reduce_scatter | solution.py:310
  343.1 255.8 %all-reduce.7.cloned.1.call-start = ((), (), s32[]{:S(2)}) async-start(), calls=%async_computation.23 | async-start | bytes 3162112 | tf_op jit(solution)/shard_map/psum | solution.py:80
  344.4 2.7 copy-start.5
  344.4 2.7 copy-start.12
  598.9 6.7 %copy-start.24 = (bf16[128,1376]{0,1:T(8,128)(2,1)S(1)}, bf16[128,1376]{0,1:T(8,128)(2,1)}, u32[]{:S(2)}) copy-start(bf16[128,1376]{0,1:T(8,128)(2,1)} %get-tuple-element.275) | copy-start | bytes 1056772
  598.9 7.6 %copy-start.23 = (bf16[128,1376]{0,1:T(8,128)(2,1)S(1)}, bf16[128,1376]{0,1:T(8,128)(2,1)}, u32[]{:S(2)}) copy-start(bf16[128,1376]{0,1:T(8,128)(2,1)} %get-tuple-element.276) | copy-start | bytes 1056772
  602.2 5.1 copy-start.22
  (7 other events, 6.6 us)
Sparse Core Ops, SparseCore 0:
  40.0 36.5 all-gather.16
  81.4 31.7 all-gather.8
  114.8 33.6 all-gather.10
  149.9 33.2 all-gather.12
  184.6 32.3 all-gather.14
  286.5 26.2 reduce-scatter.13
  315.1 25.7 reduce-scatter.15
  343.2 31.9 reduce-scatter.27
  377.5 32.1 reduce-scatter.29
  412.4 20.6 reduce-scatter.23
  435.4 31.1 reduce-scatter.25
  469.2 20.6 reduce-scatter.17
  492.7 20.1 reduce-scatter.19
  515.6 20.1 reduce-scatter.21
  539.8 59.1 all-reduce.6
where the time goes:
time: 617 us; the launch traced here: 615 us
  waiting for transfers between devices  327 us (53%)
  blocking collectives  116 us (19%)
  matrix products  104 us (17%)
  local copies, waits for them, and re-layouts  30.9 us (5%)
  other arithmetic  20.6 us (3%)
  between operations  15.1 us (2%)
    unnamed x17, waiting for transfers between devices  62.9 us
    psum x1, waiting for transfers between devices, replica_all(): lax.psum(parts[2].astype(jnp.bfloat16), 'rep').astype(jnp.float32)  38.6 us
    reduce_scatter x1, waiting for transfers between devices, flat_body(): lax.psum_scatter(contract_rows(columns, cot_low).astype(jnp.bfloat16), 'g...  33.5 us
    all_gather x1, waiting for transfers between devices, fetch_mlp(): lax.all_gather(w_up, 'grp', axis=0, tiled=True)  31.7 us
    all_gather x1, waiting for transfers between devices, fetch_mlp(): lax.all_gather(w_down, 'grp', axis=0, tiled=True)  30.8 us
    dot_general x16, matrix products, masked_scores(): jnp.einsum('bqgd,bjd->bgqj', query_head, key_head, preferred_element_type...  25.2 us
    reduce_scatter x1, waiting for transfers between devices, flat_body(): lax.psum_scatter(query_term.astype(jnp.bfloat16), 'grp', scatter_dimensio...  23.4 us
    reduce_scatter x1, waiting for transfers between devices, flat_body(): lax.psum_scatter(value_delta_all.astype(jnp.bfloat16), 'grp', scatter_dim...  23.2 us
  transfers between devices with their start and end apart: 15, of which 13 were waited for; matrix products, arithmetic and copies ran while one was open for 12% of the time, Pallas kernels for 0%

commit v1 on v0

--- a/solution.py
+++ b/solution.py
@@ -9,6 +9,27 @@
 HD = 64
 EPSILON = 1e-05
 NEGATIVE = -1e30
+
+
+def collect(shard, axis, dim):
+    length, index, rows = (lax.axis_size(axis), lax.axis_index(axis), shard.shape[dim])
+    right = [(i, (i + 1) % length) for i in range(length)]
+    left = [(i, (i - 1) % length) for i in range(length)]
+    whole = jnp.zeros((*shard.shape[:dim], length * rows, *shard.shape[dim + 1 :]), shard.dtype)
+    whole = lax.dynamic_update_slice_in_dim(whole, shard, index * rows, axis=dim)
+    from_left = from_right = shard
+    halfway = length // 2
+    for hop in range(1, halfway + 1):
+        from_left = lax.ppermute(from_left, axis, right)
+        whole = lax.dynamic_update_slice_in_dim(
+            whole, from_left, (index - hop) % length * rows, axis=dim
+        )
+        if hop < length - halfway:
+            from_right = lax.ppermute(from_right, axis, left)
+            whole = lax.dynamic_update_slice_in_dim(
+                whole, from_right, (index + hop) % length * rows, axis=dim
+            )
+    return whole
 
 
 def norm_scale(values):
@@ -57,7 +78,7 @@
 def fetch_attention(norm1_gain, w_query, w_key, w_value, w_out):
     return (
         lax.all_gather(norm1_gain, "grp", axis=0, tiled=True),
-        lax.all_gather(w_query, "grp", axis=0, tiled=True),
+        collect(w_query, "grp", 0),
         lax.all_gather(w_key, "grp", axis=0, tiled=True),
         lax.all_gather(w_value, "grp", axis=0, tiled=True),
         lax.all_gather(w_out, "grp", axis=0, tiled=True),

time: 617 us -> 613 us (level)
  blocking collectives: 116 us -> 95.6 us
  waiting for transfers between devices: 327 us -> 336 us
    all_gather x1 -> x0, blocking collectives: 19.2 us -> none  [fetch_attention(): lax.all_gather(w_query, 'grp', axis=0, tiled=True)]
    ppermute x0 -> x3, waiting for transfers between devices: none -> 10.2 us  [the longest x2 10.2 us: collect(): from_left = lax.ppermute(from_left, axis, right)]
    unnamed x89 -> x88, local copies, waits for them, and re-layouts: 18.3 us -> 18.5 us
  transfers between devices with their start and end apart: 15 -> 18, of which waited for: 13 -> 14; matrix products, arithmetic and copies ran while one was open for 12% -> 12% of each run, Pallas kernels for 0% -> 0%
where the time goes in v1:
time: 613 us; the launch traced here: 611 us
  waiting for transfers between devices  336 us (55%)
  matrix products  105 us (17%)
  blocking collectives  95.6 us (16%)
  local copies, waits for them, and re-layouts  31.5 us (5%)
  other arithmetic  20.6 us (3%)
  between operations  15.2 us (2%)
    unnamed x17, waiting for transfers between devices  62.2 us
    psum x1, waiting for transfers between devices, replica_all(): lax.psum(parts[2].astype(jnp.bfloat16), 'rep').astype(jnp.float32)  38.6 us
    reduce_scatter x1, waiting for transfers between devices, flat_body(): lax.psum_scatter(contract_rows(columns, cot_low).astype(jnp.bfloat16), 'g...  33.5 us
    all_gather x1, waiting for transfers between devices, fetch_mlp(): lax.all_gather(w_up, 'grp', axis=0, tiled=True)  31.6 us
    all_gather x1, waiting for transfers between devices, fetch_mlp(): lax.all_gather(w_down, 'grp', axis=0, tiled=True)  30.8 us
    dot_general x16, matrix products, masked_scores(): jnp.einsum('bqgd,bjd->bgqj', query_head, key_head, preferred_element_type...  25.2 us
    reduce_scatter x1, waiting for transfers between devices, flat_body(): lax.psum_scatter(query_term.astype(jnp.bfloat16), 'grp', scatter_dimensio...  23.3 us
    reduce_scatter x1, waiting for transfers between devices, flat_body(): lax.psum_scatter(value_delta_all.astype(jnp.bfloat16), 'grp', scatter_dim...  23.2 us
  transfers between devices with their start and end apart: 18, of which 14 were waited for; matrix products, arithmetic and copies ran while one was open for 12% of the time, Pallas kernels for 0%

profile of v1, /device:TPU:0, one launch (start us, length us, event | category | flops | bytes accessed | tf_op | source)
XLA Modules:
  0.0 610.6 jit_solution(10199262282425821649)
XLA Ops:
  7.2 3.1 collective-permute-start
  10.3 2.1 collective-permute-start.1
  12.4 17.3 %all_gather.39 = bf16[512,512]{1,0:T(8,128)(2,1)S(1)} all-gather(bf16[128,512]{1,0:T(8,128)(2,1)} %param.23), channel_id=1, replica_groups=mesh['rep'=8,'grp'=4] {'grp'}, dimensions={0}, use_global_device_ids=true | all-gather | bytes 655360 | tf_op jit(solution)/shard_map/all_gather | solution.py:83
  29.7 10.5 %all-gather.1 = bf16[4,1,128]{2,1,0:T(2,128)(2,1)S(1)} all-gather(bf16[1,1,128]{2,1,0:T(2,128)(2,1)} %bitcast.347), channel_id=1, replica_groups=mesh['rep'=8,'grp'=4] {'grp'}, dimensions={0}, use_global_device_ids=true | all-gather | bytes 1280 | tf_op jit(solution)/shard_map/all_gather | solution.py:80
  41.4 2.1 convolution_convert_fusion.8
  43.5 19.2 %all_gather.41 = bf16[512,512]{1,0:T(8,128)(2,1)S(1)} all-gather(bf16[128,512]{1,0:T(8,128)(2,1)S(1)} %copy-done.26), channel_id=1, replica_groups=mesh['rep'=8,'grp'=4] {'grp'}, dimensions={0}, use_global_device_ids=true | all-gather | bytes 655360 | tf_op jit(solution)/shard_map/all_gather | solution.py:82
  64.3 10.2 %collective-permute-done.2 = bf16[128,512]{1,0:T(8,128)(2,1)S(1)} collective-permute-done((bf16[128,512]{1,0:T(8,128)(2,1)S(1)}, bf16[128,512]{1,0:T(8,128)(2,1)S(1)}, u32[]{:S(2)}, u32[]{:S(2)}) %collective-permute-start.2) | collective-permute-done | bytes 131104 | tf_op jit(solution)/shard_map/ppermute | solution.py:23
  79.0 18.0 %all_gather.43 = bf16[512,512]{1,0:T(8,128)(2,1)S(1)} all-gather(bf16[128,512]{1,0:T(8,128)(2,1)S(1)} %copy-done.27), channel_id=1, replica_groups=mesh['rep'=8,'grp'=4] {'grp'}, dimensions={0}, use_global_device_ids=true | all-gather | bytes 655360 | tf_op jit(solution)/shard_map/all_gather | solution.py:84
  96.9 10.1 %all-gather.2 = bf16[4,1,128]{2,1,0:T(2,128)(2,1)S(1)} all-gather(bf16[1,1,128]{2,1,0:T(2,128)(2,1)S(1)} %bitcast.348), channel_id=1, replica_groups=mesh['rep'=8,'grp'=4] {'grp'}, dimensions={0}, use_global_device_ids=true | all-gather | bytes 1280 | tf_op jit(solution)/shard_map/all_gather | solution.py:90
  107.7 2.3 copy.51
  110.0 2.0 copy.57
  112.1 2.7 copy.58
  114.8 26.1 %while.30 = (s32[]{:T(128)}, bf16[8,1,256,1,64]{2,4,3,1,0:T(8,128)(2,1)}, f32[8,1,1,256,1]{3,4,2,1,0:T(1,128)}, bf16[8,1,1024,64]{3,2,1,0:T(8,128)(2,1)S(1)}, bf...) while((s32[]{:T(128)}, ...), condition=%wide.region_4.5_spmd.clone.clone, body=%wide.region_1.4_spmd.clone.sunk.clone | while | flops 71040768 | bytes 3783017 | solution.py:191
  145.3 3.0 fusion.105
  148.4 31.6 %all-gather.13.cloned.1.call-done = bf16[512,1376]{0,1:T(8,128)(2,1)} async-done(((bf16[128,1376]{0,1:T(8,128)(2,1)}), bf16[512,1376]{0,1:T(8,128)(2,1)}) %all-gather.13.cloned.1.call-update) | async-done | bytes 1409040 | tf_op jit(solution)/shard_map/all_gather | solution.py:92
  180.0 3.0 fusion.106
  183.0 30.8 %all-gather.15.cloned.1.call-done = bf16[1376,512]{1,0:T(8,128)(2,1)} async-done(((bf16[344,512]{1,0:T(8,128)(2,1)}), bf16[1376,512]{1,0:T(8,128)(2,1)}) %all-gather.15.cloned.1.call-update) | async-done | bytes 1409040 | tf_op jit(solution)/shard_map/all_gather | solution.py:93
  213.8 4.0 multiply_convert_fusion.1
  223.0 60.3 %while.31 = (s32[]{:T(128)}, f32[8,1,256,1,64]{2,4,3,1,0:T(8,128)S(1)}, bf16[8,1,1024,64]{2,3,1,0:T(8,128)(2,1)}, bf16[8,1,1024,64]{2,3,1,0:T(8,128)(2,1)}, bf16...) while((s32[]{:T(128)}, ...), condition=%wide.region_9.10_spmd.clone.clone, body=%wide.region_7.9_spmd.clone.sunk.clone | while | flops 172048128 | bytes 9384321 | solution.py:277
  224.9 1.7 multiply_reduce_fusion.6
  227.9 1.7 fusion.190
  235.5 1.7 fusion.190
  240.0 1.6 multiply_reduce_fusion.6
  243.0 1.7 fusion.190
  250.5 1.7 fusion.190
  258.1 1.7 fusion.190
  265.7 1.7 fusion.190
  273.1 1.7 fusion.190
  280.6 1.7 fusion.190
  287.4 1.7 convolution_convert_fusion
  294.5 15.3 %reduce-scatter.14.cloned.1.call-done = bf16[1,256,512]{1,2,0:T(8,128)(2,1)} async-done(((bf16[1,1024,512]{1,2,0:T(8,128)(2,1)}), bf16[1,256,512]{1,2,0:T(8,128)(2,1)}) %reduce-scatter.14.cloned.1.call-update) | async-done | bytes 262160 | tf_op jit(solution)/shard_map/reduce_scatter | solution.py:283
  314.7 23.2 %reduce-scatter.16.cloned.1.call-done = bf16[1,256,512]{1,2,0:T(8,128)(2,1)} async-done(((bf16[1,1024,512]{1,2,0:T(8,128)(2,1)}), bf16[1,256,512]{1,2,0:T(8,128)(2,1)}) %reduce-scatter.16.cloned.1.call-update) | async-done | bytes 262160 | tf_op jit(solution)/shard_map/reduce_scatter | solution.py:286
  337.9 2.2 convolution_convert_fusion.4
  341.4 2.6 fusion.64
  345.2 27.0 %reduce-scatter.28.cloned.1.call-done = bf16[128,1376]{1,0:T(8,128)(2,1)} async-done(((bf16[512,1376]{1,0:T(8,128)(2,1)}), bf16[128,1376]{1,0:T(8,128)(2,1)}) %reduce-scatter.28.cloned.1.call-update) | async-done | bytes 352272
  372.1 1.9 copy.69
  374.1 32.6 %reduce-scatter.30.cloned.1.call-done = bf16[128,1376]{1,0:T(8,128)(2,1)} async-done(((bf16[512,1376]{1,0:T(8,128)(2,1)}), bf16[128,1376]{1,0:T(8,128)(2,1)}) %reduce-scatter.30.cloned.1.call-update) | async-done | bytes 352272
  406.7 1.9 copy.71
  408.6 20.9 %reduce-scatter.24.cloned.1.call-done = bf16[128,512]{1,0:T(8,128)(2,1)} async-done(((bf16[512,512]{1,0:T(8,128)(2,1)}), bf16[128,512]{1,0:T(8,128)(2,1)}) %reduce-scatter.24.cloned.1.call-update) | async-done | bytes 131088 | tf_op jit(solution)/shard_map/reduce_scatter | solution.py:334
  429.4 33.5 %reduce-scatter.26.cloned.1.call-done = bf16[344,512]{1,0:T(8,128)(2,1)} async-done(((bf16[1376,512]{1,0:T(8,128)(2,1)}), bf16[344,512]{1,0:T(8,128)(2,1)}) %reduce-scatter.26.cloned.1.call-update) | async-done | bytes 352272 | tf_op jit(solution)/shard_map/reduce_scatter | solution.py:229
  462.9 23.3 %reduce-scatter.18.cloned.1.call-done = bf16[128,512]{1,0:T(8,128)(2,1)} async-done(((bf16[512,512]{1,0:T(8,128)(2,1)}), bf16[128,512]{1,0:T(8,128)(2,1)}) %reduce-scatter.18.cloned.1.call-update) | async-done | bytes 131088 | tf_op jit(solution)/shard_map/reduce_scatter | solution.py:325
  486.3 23.0 %reduce-scatter.20.cloned.1.call-done = bf16[128,512]{1,0:T(8,128)(2,1)} async-done(((bf16[512,512]{1,0:T(8,128)(2,1)}), bf16[128,512]{1,0:T(8,128)(2,1)}) %reduce-scatter.20.cloned.1.call-update) | async-done | bytes 131088 | tf_op jit(solution)/shard_map/reduce_scatter | solution.py:328
  509.2 22.2 %reduce-scatter.22.cloned.1.call-done = bf16[128,512]{1,0:T(8,128)(2,1)} async-done(((bf16[512,512]{1,0:T(8,128)(2,1)}), bf16[128,512]{1,0:T(8,128)(2,1)}) %reduce-scatter.22.cloned.1.call-update) | async-done | bytes 131088 | tf_op jit(solution)/shard_map/reduce_scatter | solution.py:331
  533.3 8.6 %all-reduce.4 = (bf16[512]{0:T(512)(128)(2,1)S(1)}, bf16[512]{0:T(512)(128)(2,1)S(1)}) all-reduce(bf16[512]{0:T(512)(128)(2,1)S(1)} %get-tuple-element.225, bf16[512]{0:T(512)(128)(2,1)S(1)} %copy-done.29), channel_id=5, replica_groups=mesh['rep'=8,'grp'=4] {'grp'}, use_global_device_ids=true, to_apply=%region_14.15.clone | all-reduce | flops 1024 | bytes 4096
  542.1 12.0 %all-reduce.2 = (bf16[128]{0:T(256)(128)(2,1)S(1)}, bf16[128]{0:T(256)(128)(2,1)S(1)}) all-reduce(bf16[128]{0:T(256)(128)(2,1)S(1)} %dynamic-slice.1, bf16[128]{0:T(256)(128)(2,1)S(1)} %dynamic-slice.3), channel_id=1, replica_groups=mesh['rep'=8,'grp'=4] {'rep'}, use_global_device_ids=true, to_apply=%region_15.16 | all-reduce | flops 256 | bytes 1024 | tf_op jit(solution)/shard_map/psum | solution.py:99
  556.1 38.6 %all-reduce.7.cloned.1.call-done = (bf16[128,512]{1,0:T(8,128)(2,1)}, bf16[128,512]{1,0:T(8,128)(2,1)}, bf16[128,512]{1,0:T(8,128)(2,1)}, bf16[128,512]{1,0:T(8,...) async-done(((bf16[128,512]{1,0:T(8,128)(2,1)}, bf16[128,512]{1,0:T(8,128)(2,1)}, bf16[128,512]{1,0:T(8,128)(2,1)}, ...) | async-done | bytes 1581072 | tf_op jit(solution)/shard_map/psum | solution.py:101
  594.7 1.7 convert_element_type.288
  598.0 1.7 convert_element_type.292
  (264 shorter events, 112.4 us)
Async XLA Ops:
  7.2 36.3 %copy-start.26 = (bf16[128,512]{1,0:T(8,128)(2,1)S(1)}, bf16[128,512]{1,0:T(8,128)(2,1)}, u32[]{:S(2)}) copy-start(bf16[128,512]{1,0:T(8,128)(2,1)} %param.22) | copy-start | bytes 393220
  7.2 55.5 %copy-start.30 = (s32[1,256]{1,0:T(1,128)S(1)}, s32[1,256]{1,0:T(1,128)}, u32[]{:S(2)}) copy-start(s32[1,256]{1,0:T(1,128)} %param.19) | copy-start | bytes 3076
  7.2 100.5 %all-gather.17.cloned.1.call-start = ((), (), s32[]{:S(2)}) async-start(), calls=%async_computation.20 | async-start | bytes 1310720 | tf_op jit(solution)/shard_map/all_gather | solution.py:154
  7.2 56.6 %collective-permute-start = (bf16[128,512]{1,0:T(8,128)(2,1)}, bf16[128,512]{1,0:T(8,128)(2,1)S(1)}, u32[]{:S(2)}, u32[]{:S(2)}) collective-permute-start(bf16[128,512]{1,0:T(8,128)(2,1)} %param.21), channel_id=1, source_target_pairs={{0,1},{1,2},{2,3},{3,0},{4,5},{5,6},{6,7},{7,4},{8,9},{9,10},{10,1... | collective-permute-start | bytes 393224 | tf_op jit(solution)/shard_map/ppermute | solution.py:23
  10.3 53.8 %collective-permute-start.1 = (bf16[128,512]{1,0:T(8,128)(2,1)}, bf16[128,512]{1,0:T(8,128)(2,1)S(1)}, u32[]{:S(2)}, u32[]{:S(2)}) collective-permute-start(bf16[128,512]{1,0:T(8,128)(2,1)} %param.21), channel_id=1, source_target_pairs={{0,3},{1,0},{2,1},{3,2},{4,7},{5,4},{6,5},{7,6},{8,11},{9,8},{10,9... | collective-permute-start | bytes 393224 | tf_op jit(solution)/shard_map/ppermute | solution.py:28
  29.7 11.6 %copy-start.13 = (bf16[512,512]{1,0:T(8,128)(2,1)}, bf16[512,512]{1,0:T(8,128)(2,1)S(1)}, u32[]{:S(2)}) copy-start(bf16[512,512]{1,0:T(8,128)(2,1)S(1)} %all_gather.39) | copy-start | bytes 1572868
  41.3 21.8 %copy-start = (bf16[1,256,512]{2,1,0:T(8,128)(2,1)S(1)}, bf16[1,256,512]{2,1,0:T(8,128)(2,1)}, u32[]{:S(2)}) copy-start(bf16[1,256,512]{2,1,0:T(8,128)(2,1)} %param.17) | copy-start | bytes 786436
  43.5 20.1 %copy-start.28 = (bf16[128,512]{1,0:T(8,128)(2,1)S(1)}, bf16[128,512]{1,0:T(8,128)(2,1)}, u32[]{:S(2)}) copy-start(bf16[128,512]{1,0:T(8,128)(2,1)} %param.21) | copy-start | bytes 393220
  43.5 68.6 %all-gather.9.cloned.1.call-start = ((), (), s32[]{:S(2)}) async-start(), calls=%async_computation.9 | async-start | bytes 1310720 | tf_op jit(solution)/shard_map/all_gather | solution.py:153
  63.1 12.0 %copy-start.24 = (f32[256,32]{0,1:T(8,128)}, f32[256,32]{0,1:T(8,128)S(1)}, u32[]{:S(2)}) copy-start(f32[256,32]{0,1:T(8,128)S(1)} %get-tuple-element.300) | copy-start | bytes 98308
  64.0 10.5 %collective-permute-start.2 = (bf16[128,512]{1,0:T(8,128)(2,1)S(1)}, bf16[128,512]{1,0:T(8,128)(2,1)S(1)}, u32[]{:S(2)}, u32[]{:S(2)}) collective-permute-start(bf16[128,512]{1,0:T(8,128)(2,1)S(1)} %collective-permute-done), channel_id=1, source_target_pairs={{0,1},{1,2},{2,3},{3,0},{4,5},{5,6},{6,7},{7,4},{8,9},{9,10},{10,1... | collective-permute-start | bytes 393224 | tf_op jit(solution)/shard_map/ppermute | solution.py:23
  75.5 3.4 copy-start.33
  75.5 3.5 copy-start.27
  75.5 21.4 %copy-start.32 = (bf16[128]{0:T(256)(128)(2,1)S(1)}, bf16[128]{0:T(256)(128)(2,1)}, u32[]{:S(2)}) copy-start(bf16[128]{0:T(256)(128)(2,1)} %param.25) | copy-start | bytes 772
  76.3 69.1 %all-gather.11.cloned.1.call-start = ((), (), s32[]{:S(2)}) async-start(), calls=%async_computation.10 | async-start | bytes 1761280 | tf_op jit(solution)/shard_map/all_gather | solution.py:91
  77.0 103.0 %all-gather.13.cloned.1.call-start = ((), (), s32[]{:S(2)}) async-start(), calls=%async_computation.11 | async-start | bytes 1761280 | tf_op jit(solution)/shard_map/all_gather | solution.py:92
  77.6 136.3 %all-gather.15.cloned.1.call-start = ((), (), s32[]{:S(2)}) async-start(), calls=%async_computation.12 | async-start | bytes 1761280 | tf_op jit(solution)/shard_map/all_gather | solution.py:93
  78.2 231.6 %reduce-scatter.14.cloned.1.call-start = ((), (), s32[]{:S(2)}) async-start(), calls=%async_computation.13 | async-start | bytes 1310720 | tf_op jit(solution)/shard_map/reduce_scatter | solution.py:283
  96.9 45.3 %copy-start.6 = (bf16[512,512]{1,0:T(8,128)(2,1)}, bf16[512,512]{1,0:T(8,128)(2,1)S(1)}, u32[]{:S(2)}) copy-start(bf16[512,512]{1,0:T(8,128)(2,1)S(1)} %all_gather.43) | copy-start | bytes 1572868
  140.9 1.3 copy-start.3
  140.9 7.5 %copy-start.34 = (s32[256]{0:T(256)}, s32[256]{0:T(256)S(1)}, u32[]{:S(2)}) copy-start(s32[256]{0:T(256)S(1)} %get-tuple-element.650) | copy-start | bytes 3076
  140.9 7.5 %copy-start.37 = (pred[256]{0:T(512)(128)(4,1)}, pred[256]{0:T(512)(128)(4,1)S(1)}, u32[]{:S(2)}) copy-start(pred[256]{0:T(512)(128)(4,1)S(1)} %get-tuple-element.651) | copy-start | bytes 772
  148.4 65.5 %copy-start.15 = (bf16[1,256,512]{2,1,0:T(8,128)(2,1)S(1)}, bf16[1,256,512]{2,1,0:T(8,128)(2,1)}, u32[]{:S(2)}) copy-start(bf16[1,256,512]{2,1,0:T(8,128)(2,1)} %param.29) | copy-start | bytes 786436
  183.0 34.8 %copy-start.2 = (bf16[512,1376]{0,1:T(8,128)(2,1)S(1)}, bf16[512,1376]{0,1:T(8,128)(2,1)}, u32[]{:S(2)}) copy-start(bf16[512,1376]{0,1:T(8,128)(2,1)} %all-gather.11.cloned.1.call-done) | copy-start | bytes 4227076
  217.8 3.1 copy-start.8
  217.8 3.1 copy-start.10
  217.8 1.9 copy-start.1
  220.9 1.5 copy-start.31
  220.9 1.5 copy-start.35
  221.0 1.5 copy-start.38
  283.3 54.6 %reduce-scatter.16.cloned.1.call-start = ((), (), s32[]{:S(2)}) async-start(), calls=%async_computation.14 | async-start | bytes 1310720 | tf_op jit(solution)/shard_map/reduce_scatter | solution.py:286
  284.1 88.1 %reduce-scatter.28.cloned.1.call-start = ((), (), s32[]{:S(2)}) async-start(), calls=%async_computation.21 | async-start | bytes 1802240
  287.3 119.3 %reduce-scatter.30.cloned.1.call-start = ((), (), s32[]{:S(2)}) async-start(), calls=%async_computation.22 | async-start | bytes 1802240
  290.6 2.1 copy-start.9
  290.6 2.1 copy-start.17
  290.6 138.8 %reduce-scatter.24.cloned.1.call-start = ((), (), s32[]{:S(2)}) async-start(), calls=%async_computation.18 | async-start | bytes 655360 | tf_op jit(solution)/shard_map/reduce_scatter | solution.py:334
  292.7 170.2 %reduce-scatter.26.cloned.1.call-start = ((), (), s32[]{:S(2)}) async-start(), calls=%async_computation.19 | async-start | bytes 1761280 | tf_op jit(solution)/shard_map/reduce_scatter | solution.py:229
  294.4 16.4 %copy-start.25 = (f32[256,32]{0,1:T(8,128)S(1)}, f32[256,32]{0,1:T(8,128)}, u32[]{:S(2)}) copy-start(f32[256,32]{0,1:T(8,128)} %copy-done.24) | copy-start | bytes 98308
  294.4 191.8 %reduce-scatter.18.cloned.1.call-start = ((), (), s32[]{:S(2)}) async-start(), calls=%async_computation.15 | async-start | bytes 655360 | tf_op jit(solution)/shard_map/reduce_scatter | solution.py:325
  313.3 195.9 %reduce-scatter.20.cloned.1.call-start = ((), (), s32[]{:S(2)}) async-start(), calls=%async_computation.16 | async-start | bytes 655360 | tf_op jit(solution)/shard_map/reduce_scatter | solution.py:328
  313.4 26.8 %copy-start.36 = (u32[32]{0:T(128)S(1)}, u32[32]{0:T(128)}, u32[]{:S(2)}) copy-start(u32[32]{0:T(128)} %constant.122) | copy-start | bytes 388
  314.6 216.8 %reduce-scatter.22.cloned.1.call-start = ((), (), s32[]{:S(2)}) async-start(), calls=%async_computation.17 | async-start | bytes 655360 | tf_op jit(solution)/shard_map/reduce_scatter | solution.py:331
  340.1 254.6 %all-reduce.7.cloned.1.call-start = ((), (), s32[]{:S(2)}) async-start(), calls=%async_computation.23 | async-start | bytes 3162112 | tf_op jit(solution)/shard_map/psum | solution.py:101
  345.2 186.3 %copy-start.14 = (bf16[512,512]{1,0:T(8,128)(2,1)S(1)}, bf16[512,512]{1,0:T(8,128)(2,1)}, u32[]{:S(2)}) copy-start(bf16[512,512]{1,0:T(8,128)(2,1)} %copy-done.13) | copy-start | bytes 1572868
  345.2 186.3 %copy-start.18 = (bf16[1,256,512]{1,2,0:T(8,128)(2,1)S(1)}, bf16[1,256,512]{1,2,0:T(8,128)(2,1)}, u32[]{:S(2)}) copy-start(bf16[1,256,512]{1,2,0:T(8,128)(2,1)} %reduce-scatter.16.cloned.1.call-done) | copy-start | bytes 786436
  594.7 6.7 %copy-start.23 = (bf16[128,1376]{0,1:T(8,128)(2,1)S(1)}, bf16[128,1376]{0,1:T(8,128)(2,1)}, u32[]{:S(2)}) copy-start(bf16[128,1376]{0,1:T(8,128)(2,1)} %get-tuple-element.275) | copy-start | bytes 1056772
  594.7 7.6 %copy-start.22 = (bf16[128,1376]{0,1:T(8,128)(2,1)S(1)}, bf16[128,1376]{0,1:T(8,128)(2,1)}, u32[]{:S(2)}) copy-start(bf16[128,1376]{0,1:T(8,128)(2,1)} %get-tuple-element.276) | copy-start | bytes 1056772
  598.0 5.1 copy-start.21
  (9 other events, 8.8 us)
Sparse Core Ops, SparseCore 0:
  43.6 32.7 all-gather.16
  78.5 31.0 all-gather.8
  111.2 34.0 all-gather.10
  146.7 33.2 all-gather.12
  181.4 32.3 all-gather.14
  283.4 26.2 reduce-scatter.13
  312.1 25.7 reduce-scatter.15
  340.2 31.8 reduce-scatter.27
  374.5 32.1 reduce-scatter.29
  408.8 20.6 reduce-scatter.23
  431.8 31.1 reduce-scatter.25
  465.6 20.5 reduce-scatter.17
  489.1 20.0 reduce-scatter.19
  511.4 20.0 reduce-scatter.21
  535.5 59.1 all-reduce.6
